TPU v7x, 256 devices: a whole 4x4x8 slice. The times are simulated.
256 devices in a mesh: expert: 8 (over x, core), replica: 32 (over y, z).
Axes of the slice: x: 4, y: 4, z: 8, core: 2. Of those that a mesh axis runs over, the one named last changes fastest.
Arguments:
- tokens: bfloat16 [1536, 4096], P(('expert', 'replica')), may hold values from -6 to 6
- out_grad: bfloat16 [1536, 4096], P(('expert', 'replica')), may hold values from -2.5 to 2.5
- expert_ids: int32 [1536, 2], P(('expert', 'replica')), may hold values from 0 to 7, all different within a row; in each aligned block of 6 rows (0 to 5, 6 to 11, ...) at most 2 rows name the same one
- gates: float32 [1536, 2], P(('expert', 'replica')), may hold values from 0.1 to 1
- w_gate: bfloat16 [8, 7168, 4096], P('expert', 'replica'), may hold values from -0.09375 to 0.09375
- w_up: bfloat16 [8, 7168, 4096], P('expert', 'replica'), may hold values from -0.09375 to 0.09375
- w_down: bfloat16 [8, 7168, 4096], P('expert', 'replica'), may hold values from -0.0625 to 0.0625
Outputs:
- gate_grad: float32 [1536, 2], P(('expert', 'replica'))
- input_grad: bfloat16 [1536, 4096], P(('expert', 'replica'))
- grad_gate: bfloat16 [8, 7168, 4096], P('expert', 'replica')
- grad_up: bfloat16 [8, 7168, 4096], P('expert', 'replica')
- grad_down: bfloat16 [8, 7168, 4096], P('expert', 'replica')
Inputs may be any that keep to these rules, and one draw needn't show every extreme that they name: `expert_ids`: each row names 2 different experts; among the rows of one device no expert is named more than 2 times.
All inputs are finite; a program needn't handle non-finite values.
Results may differ from a plain program's by a relative error of at most 0.02.
Values may be sent and summed in bfloat16 or wider, within the bound.
No kernel may reach another device: no remote copies, remote signals or barrier semaphores. Data moves between devices by JAX's collectives and lax.ppermute only.
A program may use at most 128 MiB of HBM per device.

v0:
```python
import jax
import jax.numpy as jnp
from jax import lax
from jax.sharding import Mesh
from jax.sharding import PartitionSpec as P

REPLICA = ("replica_0", "replica_1")
EXPERT_REPLICA = ("expert", "replica_0", "replica_1")


def split_up(value, dim, peers):
    shape = value.shape
    tiles = value.reshape(*shape[:dim], peers, shape[dim] // peers, *shape[dim + 1 :])
    return jnp.moveaxis(tiles, dim, 0)


def sum_at_owner(value, axis, dim):
    peers = lax.axis_size(axis)
    tiles = lax.all_to_all(split_up(value, dim, peers), axis, 0, 0, tiled=True)
    return jnp.sum(tiles, axis=0)


def own_rows(terms, axes):
    running = terms.astype(jnp.bfloat16)
    for axis in axes:
        running = lax.psum_scatter(running, axis, scatter_dimension=0, tiled=True)
    return running.astype(jnp.float32)


def on_device(tokens, out_grad, expert_ids, gates, w_gate, w_up, w_down):
    token_count = tokens.shape[0]
    fan_out = expert_ids.shape[1]
    model_width = tokens.shape[1]
    owners = lax.axis_size("expert")
    capacity = max(2, 4 * token_count * fan_out // (3 * owners))
    slot_count = owners * capacity
    flat_ids = expert_ids.reshape(-1)
    sequence_pos = jnp.arange(token_count * fan_out, dtype=jnp.int32)
    earlier = sequence_pos[None, :] < sequence_pos[:, None]
    same_expert = flat_ids[:, None] == flat_ids[None, :]
    slot_rank = jnp.sum(jnp.logical_and(same_expert, earlier), axis=1)
    target = flat_ids * capacity + slot_rank
    token_hot = (target[:, None] == jnp.arange(slot_count, dtype=jnp.int32)[None, :]).astype(
        jnp.float32
    )
    token_hot = token_hot.reshape(token_count, fan_out, slot_count)
    dispatch = jnp.sum(token_hot, axis=1).astype(jnp.bfloat16)
    slot_gate = jnp.sum(token_hot * gates[:, :, None], axis=(0, 1)).reshape(owners, capacity)
    leading = (((0,), (0,)), ((), ()))
    contract = (((1,), (1,)), ((), ()))
    send_inputs = (
        lax.dot_general(dispatch, tokens, leading, preferred_element_type=jnp.float32)
        .astype(jnp.bfloat16)
        .reshape(owners, capacity, model_width)
    )
    send_grads = (
        lax.dot_general(dispatch, out_grad, leading, preferred_element_type=jnp.float32)
        .astype(jnp.bfloat16)
        .reshape(owners, capacity, model_width)
    )
    gate_weight = w_gate[0]
    up_weight = w_up[0]
    down_weight = w_down[0]
    owned = (
        lax.all_to_all(send_inputs, "expert", split_axis=0, concat_axis=0, tiled=True),
        lax.all_to_all(send_grads, "expert", split_axis=0, concat_axis=0, tiled=True),
        lax.all_to_all(
            slot_gate.astype(jnp.bfloat16), "expert", split_axis=0, concat_axis=0, tiled=True
        ).astype(slot_gate.dtype),
    )
    column_inputs, column_grads, column_gates = (
        lax.all_gather(owned[0], REPLICA, axis=0, tiled=True),
        lax.all_gather(owned[1], REPLICA, axis=0, tiled=True),
        lax.all_gather(owned[2].astype(jnp.bfloat16), REPLICA, axis=0, tiled=True).astype(
            jnp.float32
        ),
    )
    gathered = column_inputs.reshape(-1, model_width)
    gate_pre = lax.dot_general(gathered, gate_weight, contract, preferred_element_type=jnp.float32)
    up_pre = lax.dot_general(gathered, up_weight, contract, preferred_element_type=jnp.float32)
    sigmoid_gate = jax.nn.sigmoid(gate_pre)
    active = gate_pre * sigmoid_gate
    hidden = (active * up_pre).astype(jnp.bfloat16)
    gathered_grad = column_grads.reshape(-1, model_width)
    row_gates = column_gates.reshape(-1)
    full_out = jnp.dot(hidden, down_weight, preferred_element_type=jnp.float32)
    partial_value = jnp.sum(gathered_grad * full_out, axis=1)
    summed_products = sum_at_owner(partial_value, REPLICA, 0)
    returned = lax.all_to_all(
        summed_products.reshape(owners, capacity), "expert", split_axis=0, concat_axis=0, tiled=True
    )
    gate_grad = jnp.sum(token_hot * returned.reshape(-1)[None, None, :], axis=2)
    scaled = (row_gates[:, None] * gathered_grad).astype(jnp.bfloat16)
    hidden_grad = lax.dot_general(scaled, down_weight, contract, preferred_element_type=jnp.float32)
    gate_pre_grad = (
        hidden_grad * up_pre * sigmoid_gate * (1.0 + gate_pre * (1.0 - sigmoid_gate))
    ).astype(jnp.bfloat16)
    up_pre_grad = (hidden_grad * active).astype(jnp.bfloat16)
    grad_down = lax.dot_general(hidden, scaled, leading, preferred_element_type=jnp.float32).astype(
        jnp.bfloat16
    )
    grad_gate = lax.dot_general(
        gate_pre_grad, gathered, leading, preferred_element_type=jnp.float32
    ).astype(jnp.bfloat16)
    grad_up = lax.dot_general(
        up_pre_grad, gathered, leading, preferred_element_type=jnp.float32
    ).astype(jnp.bfloat16)
    slot_grad = own_rows(
        jnp.dot(gate_pre_grad, gate_weight, preferred_element_type=jnp.float32)
        + jnp.dot(up_pre_grad, up_weight, preferred_element_type=jnp.float32),
        REPLICA,
    ).astype(jnp.bfloat16)
    slot_back = lax.all_to_all(
        slot_grad.reshape(owners, capacity, model_width),
        "expert",
        split_axis=0,
        concat_axis=0,
        tiled=True,
    )
    slot_back = slot_back.reshape(slot_count, model_width)
    input_grad = jnp.dot(dispatch, slot_back, preferred_element_type=jnp.float32).astype(
        jnp.bfloat16
    )
    return (gate_grad, input_grad, grad_gate[None], grad_up[None], grad_down[None])


def solution(mesh):
    torus = Mesh(
        mesh.devices.reshape(mesh.shape["expert"], 4, 8), ("expert", "replica_0", "replica_1")
    )
    in_specs = (
        P(EXPERT_REPLICA, None),
        P(EXPERT_REPLICA, None),
        P(EXPERT_REPLICA, None),
        P(EXPERT_REPLICA, None),
        P("expert", REPLICA, None),
        P("expert", REPLICA, None),
        P("expert", REPLICA, None),
    )
    out_specs = (
        P(EXPERT_REPLICA, None),
        P(EXPERT_REPLICA, None),
        P("expert", REPLICA, None),
        P("expert", REPLICA, None),
        P("expert", REPLICA, None),
    )
    return jax.shard_map(
        on_device, mesh=torus, in_specs=in_specs, out_specs=out_specs, check_vma=False
    )
```

profile of v0, /device:TPU:1, one launch (start us, length us, event | category | flops | bytes accessed | tf_op | source)
XLA Modules:
  0.0 404.9 jit_solution(4118786558378128443)
XLA Ops:
  7.2 0.9 copy.30
  8.6 1.1 convolution_convert_fusion.3
  9.8 11.5 %all_to_all.42 = bf16[8,2,4096]{2,1,0:T(2,128)(2,1)} all-to-all(bf16[8,2,4096]{2,1,0:T(2,128)(2,1)S(1)} %reshape.81), channel_id=1, replica_groups=mesh['expert'=8,'replica_0'=4,'replica_1'=8] {'expert'}, dimensions={0} | all-to-all | bytes 262144 | tf_op jit(solution)/shard_map/all_to_all | solution.py:65
  21.3 1.1 convolution_convert_fusion.4
  22.5 9.2 %all_to_all.43 = bf16[8,2,4096]{2,1,0:T(2,128)(2,1)} all-to-all(bf16[8,2,4096]{2,1,0:T(2,128)(2,1)S(1)} %reshape.80), channel_id=1, replica_groups=mesh['expert'=8,'replica_0'=4,'replica_1'=8] {'expert'}, dimensions={0} | all-to-all | bytes 262144 | tf_op jit(solution)/shard_map/all_to_all | solution.py:66
  31.7 68.7 %all-gather.6.cloned.1.call-done = bf16[256,2,4096]{2,1,0:T(2,128)(2,1)} async-done(((bf16[8,2,4096]{2,1,0:T(2,128)(2,1)}), bf16[256,2,4096]{2,1,0:T(2,128)(2,1)}) %all-gather.6.cloned.1.call-update) | async-done | bytes 4194320 | tf_op jit(solution)/shard_map/all_gather | solution.py:72
  100.4 7.2 %reshape.82 = bf16[512,4096]{1,0:T(8,128)(2,1)} reshape(bf16[256,2,4096]{2,1,0:T(2,128)(2,1)} %all-gather.6.cloned.1.call-done) | data formatting | bytes 8388608 | tf_op jit(solution)/shard_map/reshape | solution.py:78
  107.6 4.3 %fusion.12 = f32[512,224]{0,1:T(8,128)S(1)} fusion(bf16[512,4096]{1,0:T(8,128)(2,1)} %reshape.82, bf16[1,224,4096]{2,1,0:T(8,128)(2,1)} %param.11), kind=kOutput, calls=%fused_computation.22 | convolution fusion | flops 939524096 | bytes 6488064 | tf_op jit(solution)/shard_map/dot_general | solution.py:79
  112.0 2.3 multiply_convert_fusion.5
  114.3 67.3 %all-gather.4.cloned.1.call-done = bf16[256,2,4096]{2,1,0:T(2,128)(2,1)} async-done(((bf16[8,2,4096]{2,1,0:T(2,128)(2,1)}), bf16[256,2,4096]{2,1,0:T(2,128)(2,1)}) %all-gather.4.cloned.1.call-update) | async-done | bytes 4194320 | tf_op jit(solution)/shard_map/all_gather | solution.py:73
  181.6 7.6 %reshape.85 = f32[512,4096]{1,0:T(8,128)} reshape(bf16[256,2,4096]{2,1,0:T(2,128)(2,1)} %all-gather.4.cloned.1.call-done) | data formatting | bytes 12582912 | tf_op jit(solution)/shard_map/convert_element_type | solution.py:87
  189.2 5.3 %multiply_reduce_fusion = f32[512]{0:T(512)S(1)} fusion(f32[512,4096]{1,0:T(8,128)} %reshape.85, bf16[512,224]{0,1:T(8,128)(2,1)S(1)} %get-tuple-element.14, bf16[1,224,4096]{2,1,0:T(8,128)(2,1)} %param.13), kind=kOutput, calls=%fused_computation.3 | convolution fusion | flops 943717888 | bytes 10455040 | tf_op jit(solution)/shard_map/dot_general | solution.py:86
  194.6 14.5 %all_to_all.44 = f32[32,1,16]{2,1,0:T(1,128)S(1)} all-to-all(f32[32,1,16]{2,1,0:T(1,128)S(1)} %bitcast.46), channel_id=1, replica_groups=mesh['expert'=8,'replica_0'=4,'replica_1'=8] {'replica_0','replica_1'}, dimensions={0} | all-to-all | bytes 4096 | tf_op jit(solution)/shard_map/all_to_all | solution.py:19
  209.1 0.7 all_to_all.31
  209.8 8.9 %all-to-all-start.3 = ((f32[8,1,2]{2,1,0:T(1,128)}), f32[8,1,2]{2,1,0:T(1,128)S(1)}, u32[]{:S(2)}, u32[]{:S(2)}) async-start(f32[8,1,2]{2,1,0:T(1,128)} %bitcast.4), calls=%async_computation.3 | async-start | bytes 8192 | tf_op jit(solution)/shard_map/all_to_all | solution.py:89
  218.8 4.4 %all-to-all-done.3 = f32[8,1,2]{2,1,0:T(1,128)S(1)} async-done(((f32[8,1,2]{2,1,0:T(1,128)}), f32[8,1,2]{2,1,0:T(1,128)S(1)}, u32[]{:S(2)}, u32[]{:S(2)}) %all-to-all-start.3) | async-done | bytes 96 | tf_op jit(solution)/shard_map/all_to_all | solution.py:89
  224.8 7.6 %all_to_all.45 = bf16[8,1,2]{2,1,0:T(2,128)(2,1)S(1)} all-to-all(bf16[8,1,2]{2,1,0:T(2,128)(2,1)S(1)} %convert_element_type.102), channel_id=1, replica_groups=mesh['expert'=8,'replica_0'=4,'replica_1'=8] {'expert'}, dimensions={0} | all-to-all | bytes 64 | tf_op jit(solution)/shard_map/all_to_all | solution.py:67
  232.4 31.3 %all-gather = bf16[256,1,2]{2,1,0:T(2,128)(2,1)S(1)} all-gather(bf16[8,1,2]{2,1,0:T(2,128)(2,1)S(1)} %all_to_all.45), channel_id=2, replica_groups=mesh['expert'=8,'replica_0'=4,'replica_1'=8] {'replica_0','replica_1'}, dimensions={0}, use_global_device_ids=true | all-gather | bytes 1056 | tf_op jit(solution)/shard_map/all_gather | solution.py:74
  263.8 10.4 %multiply_convert_fusion.1 = bf16[256,2,4096]{2,1,0:T(2,128)(2,1)} fusion(f32[256,2]{1,0:T(8,128)S(1)} %bitcast.45, bf16[256,2,4096]{2,1,0:T(2,128)(2,1)} %all-gather.4.cloned.1.call-done), kind=kLoop, calls=%fused_computation.2 | loop fusion | flops 6291456 | bytes 8390656 | tf_op jit(solution)/shard_map/convert_element_type | solution.py:93
  274.2 7.2 %convert_element_type.91 = bf16[512,4096]{1,0:T(8,128)(2,1)} reshape(bf16[256,2,4096]{2,1,0:T(2,128)(2,1)} %multiply_convert_fusion.1) | data formatting | bytes 8388608 | tf_op jit(solution)/shard_map/convert_element_type | solution.py:93
  281.4 4.4 %multiply_convert_fusion.3 = (bf16[512,224]{0,1:T(8,128)(2,1)S(1)}, bf16[512,224]{0,1:T(8,128)(2,1)S(1)}) fusion(f32[512,224]{0,1:T(8,128)S(1)} %fusion.12, f32[512,224]{0,1:T(8,128)} %get-tuple-element.15, bf16[512,4096]{1,0:T(8,128)(2,1)} %convert_element_type.91, bf16[1,224,4096]{2,1,0:T(8,128)(2,1)} %param.13), kind=kOutput, calls=%fused_computation.24 | convolution fusion | flops 941015040 | bytes 7405568 | tf_op jit(solution)/shard_map/dot_general | solution.py:94
  285.8 1.3 fusion.10
  287.1 3.3 add_convert_fusion
  290.7 53.7 %reduce-scatter.3.cloned.1.call-done = bf16[128,4096]{1,0:T(8,128)(2,1)} async-done(((bf16[512,4096]{1,0:T(8,128)(2,1)}), bf16[128,4096]{1,0:T(8,128)(2,1)}) %reduce-scatter.3.cloned.1.call-update) | async-done | bytes 1048592 | tf_op jit(solution)/shard_map/reduce_scatter | solution.py:26
  345.6 4.5 %fusion.1 = bf16[1,224,4096]{2,1,0:T(8,128)(2,1)} fusion(bf16[512,224]{0,1:T(8,128)(2,1)S(1)} %get-tuple-element.12, bf16[512,4096]{1,0:T(8,128)(2,1)} %reshape.82), kind=kOutput, calls=%fused_computation.8 | convolution fusion | flops 940441600 | bytes 6258688 | tf_op jit(solution)/shard_map/dot_general | solution.py:105
  350.2 5.8 %fusion.2 = bf16[1,224,4096]{2,1,0:T(8,128)(2,1)} fusion(bf16[512,224]{0,1:T(8,128)(2,1)S(1)} %get-tuple-element.14, f32[512,4096]{1,0:T(8,128)} %reshape.85, f32[512]{0:T(512)S(1)} %mul.80), kind=kOutput, calls=%fused_computation.9 | convolution fusion | flops 944635904 | bytes 10455040 | tf_op jit(solution)/shard_map/dot_general | solution.py:99
  356.0 24.6 %reduce-scatter.5.cloned.1.call-done = bf16[16,4096]{1,0:T(8,128)(2,1)} async-done(((bf16[128,4096]{1,0:T(8,128)(2,1)}), bf16[16,4096]{1,0:T(8,128)(2,1)}) %reduce-scatter.5.cloned.1.call-update) | async-done | bytes 131088 | tf_op jit(solution)/shard_map/reduce_scatter | solution.py:26
  380.6 1.6 reshape.83
  382.3 10.0 %all-to-all-start.5 = ((bf16[8,2,4096]{2,1,0:T(2,128)(2,1)}), bf16[8,2,4096]{2,1,0:T(2,128)(2,1)S(1)}, u32[]{:S(2)}, u32[]{:S(2)}) async-start(bf16[8,2,4096]{2,1,0:T(2,128)(2,1)} %reshape.83), calls=%async_computation.7 | async-start | bytes 262144 | tf_op jit(solution)/shard_map/all_to_all | solution.py:113
  392.3 4.5 %fusion = bf16[1,224,4096]{2,1,0:T(8,128)(2,1)} fusion(bf16[512,224]{0,1:T(8,128)(2,1)S(1)} %get-tuple-element.13, bf16[512,4096]{1,0:T(8,128)(2,1)} %reshape.82), kind=kOutput, calls=%fused_computation.7 | convolution fusion | flops 940441600 | bytes 6258688 | tf_op jit(solution)/shard_map/dot_general | solution.py:102
  396.8 0.7 all-to-all-done.5
  397.6 0.8 convolution_convert_fusion.5
  (36 shorter events, 4.1 us)
Async XLA Ops:
  7.2 104.8 %copy-start = (bf16[1,224,4096]{2,1,0:T(8,128)(2,1)S(1)}, bf16[1,224,4096]{2,1,0:T(8,128)(2,1)}, u32[]{:S(2)}) copy-start(bf16[1,224,4096]{2,1,0:T(8,128)(2,1)} %param.12) | copy-start | bytes 5505028
  7.2 93.2 %all-gather.6.cloned.1.call-start = ((), (), s32[]{:S(2)}) async-start(), calls=%async_computation.9 | async-start | bytes 4325376 | tf_op jit(solution)/shard_map/all_gather | solution.py:72
  21.3 160.3 %all-gather.4.cloned.1.call-start = ((), (), s32[]{:S(2)}) async-start(), calls=%async_computation.8 | async-start | bytes 4325376 | tf_op jit(solution)/shard_map/all_gather | solution.py:73
  107.6 4.4 %copy-start.1 = (bf16[512,4096]{1,0:T(8,128)(2,1)S(1)}, bf16[512,4096]{1,0:T(8,128)(2,1)}, u32[]{:S(2)}) copy-start(bf16[512,4096]{1,0:T(8,128)(2,1)} %reshape.82) | copy-start | bytes 12582916
  189.2 29.6 %copy-start.3 = (f32[6,2]{0,1:T(2,128)S(1)}, f32[6,2]{0,1:T(2,128)}, u32[]{:S(2)}) copy-start(f32[6,2]{0,1:T(2,128)} %param.10) | copy-start | bytes 148
  209.8 13.5 %all-to-all-start.3 = ((f32[8,1,2]{2,1,0:T(1,128)}), f32[8,1,2]{2,1,0:T(1,128)S(1)}, u32[]{:S(2)}, u32[]{:S(2)}) async-start(f32[8,1,2]{2,1,0:T(1,128)} %bitcast.4), calls=%async_computation.3 | async-start | bytes 8192 | tf_op jit(solution)/shard_map/all_to_all | solution.py:89
  218.7 125.7 %reduce-scatter.3.cloned.1.call-start = ((), (), s32[]{:S(2)}) async-start(), calls=%async_computation.10 | async-start | bytes 5242880 | tf_op jit(solution)/shard_map/reduce_scatter | solution.py:26
  281.4 4.4 %copy-start.2 = (bf16[1,224,4096]{2,1,0:T(8,128)(2,1)S(1)}, bf16[1,224,4096]{2,1,0:T(8,128)(2,1)}, u32[]{:S(2)}) copy-start(bf16[1,224,4096]{2,1,0:T(8,128)(2,1)} %param.11) | copy-start | bytes 5505028
  290.5 90.2 %reduce-scatter.5.cloned.1.call-start = ((), (), s32[]{:S(2)}) async-start(), calls=%async_computation.11 | async-start | bytes 1179648 | tf_op jit(solution)/shard_map/reduce_scatter | solution.py:26
  382.3 15.3 %all-to-all-start.5 = ((bf16[8,2,4096]{2,1,0:T(2,128)(2,1)}), bf16[8,2,4096]{2,1,0:T(2,128)(2,1)S(1)}, u32[]{:S(2)}, u32[]{:S(2)}) async-start(bf16[8,2,4096]{2,1,0:T(2,128)(2,1)} %reshape.83), calls=%async_computation.7 | async-start | bytes 262144 | tf_op jit(solution)/shard_map/all_to_all | solution.py:113
Sparse Core Ops, SparseCore 0:
  21.4 78.9 all-gather.5
  103.0 78.5 all-gather.3
  290.6 53.7 reduce-scatter.2
  346.8 33.7 reduce-scatter.4
where the time goes:
time: 406 us; the launch traced here: 405 us
  waiting for transfers between devices  220 us (54%)
  blocking collectives  74 us (18%)
  matrix products  38.8 us (10%)
  local copies, waits for them, and re-layouts  27.3 us (7%)
  starting transfers between devices  19.3 us (5%)
  between operations  13.9 us (3%)
  other arithmetic  12.1 us (3%)
    reduce_scatter x2, waiting for transfers between devices, own_rows(): running = lax.psum_scatter(running, axis, scatter_dimension=0, tiled=True)  78.3 us
    all_gather x1, waiting for transfers between devices, on_device(): lax.all_gather(owned[0], REPLICA, axis=0, tiled=True)  68.7 us
    all_gather x1, waiting for transfers between devices, on_device(): lax.all_gather(owned[1], REPLICA, axis=0, tiled=True)  67.3 us
    all_gather x1, blocking collectives, on_device(): lax.all_gather(owned[2].astype(jnp.bfloat16), REPLICA, axis=0, tiled=True)  31.3 us
    all_to_all x1, blocking collectives, sum_at_owner(): tiles = lax.all_to_all(split_up(value, dim, peers), axis, 0, 0, tiled=True)  14.5 us
    all_to_all x1, blocking collectives, on_device(): lax.all_to_all(send_inputs, 'expert', split_axis=0, concat_axis=0, tiled=...  11.5 us
    convert_element_type x1, other arithmetic, on_device(): scaled = (row_gates[:, None] * gathered_grad).astype(jnp.bfloat16)  10.4 us
    all_to_all x1, starting transfers between devices, on_device(): lax.all_to_all(slot_grad.reshape(owners, capacity, model_width), 'expert'...  10 us
  transfers between devices with their start and end apart: 6, of which 6 were waited for; matrix products, arithmetic and copies ran while one was open for 8% of the time, Pallas kernels for 0%

commit v1 on v0

--- a/solution.py
+++ b/solution.py
@@ -6,6 +6,13 @@
 
 REPLICA = ("replica_0", "replica_1")
 EXPERT_REPLICA = ("expert", "replica_0", "replica_1")
+
+
+def swapped_in(x, name, along):
+    n_dev = lax.axis_size(name)
+    tiles = jnp.stack([x for _ in range(n_dev)])
+    tiles = lax.all_to_all(tiles, name, split_axis=0, concat_axis=0)
+    return jnp.concatenate(tiles, axis=along)
 
 
 def split_up(value, dim, peers):
@@ -71,9 +78,7 @@
     column_inputs, column_grads, column_gates = (
         lax.all_gather(owned[0], REPLICA, axis=0, tiled=True),
         lax.all_gather(owned[1], REPLICA, axis=0, tiled=True),
-        lax.all_gather(owned[2].astype(jnp.bfloat16), REPLICA, axis=0, tiled=True).astype(
-            jnp.float32
-        ),
+        swapped_in(owned[2].astype(jnp.bfloat16), REPLICA, 0).astype(jnp.float32),
     )
     gathered = column_inputs.reshape(-1, model_width)
     gate_pre = lax.dot_general(gathered, gate_weight, contract, preferred_element_type=jnp.float32)

time: 406 us -> 376 us (0.926)
  blocking collectives: 74 us -> 54.4 us
  waiting for transfers between devices: 220 us -> 210 us
    all_gather x1 -> x0, blocking collectives: 31.3 us -> none  [on_device(): lax.all_gather(owned[2].astype(jnp.bfloat16), REPLICA, axis=0, tiled=True)]
    all_to_all x0 -> x1, blocking collectives: none -> 11.6 us  [swapped_in(): tiles = lax.all_to_all(tiles, name, split_axis=0, concat_axis=0)]
    reduce_scatter x2, waiting for transfers between devices: 78.3 us -> 68.8 us  [own_rows(): running = lax.psum_scatter(running, axis, scatter_dimension=0, tiled=True)]
where the time goes in v1:
time: 376 us; the launch traced here: 375 us
  waiting for transfers between devices  210 us (56%)
  blocking collectives  54.4 us (14%)
  matrix products  38.8 us (10%)
  local copies, waits for them, and re-layouts  27.6 us (7%)
  starting transfers between devices  18.6 us (5%)
  between operations  13.9 us (4%)
  other arithmetic  11.5 us (3%)
    reduce_scatter x2, waiting for transfers between devices, own_rows(): running = lax.psum_scatter(running, axis, scatter_dimension=0, tiled=True)  68.8 us
    all_gather x1, waiting for transfers between devices, on_device(): lax.all_gather(owned[0], REPLICA, axis=0, tiled=True)  68.7 us
    all_gather x1, waiting for transfers between devices, on_device(): lax.all_gather(owned[1], REPLICA, axis=0, tiled=True)  67.3 us
    all_to_all x1, blocking collectives, sum_at_owner(): tiles = lax.all_to_all(split_up(value, dim, peers), axis, 0, 0, tiled=True)  14.5 us
    all_to_all x1, blocking collectives, swapped_in(): tiles = lax.all_to_all(tiles, name, split_axis=0, concat_axis=0)  11.6 us
    all_to_all x1, blocking collectives, on_device(): lax.all_to_all(send_inputs, 'expert', split_axis=0, concat_axis=0, tiled=...  11.5 us
    convert_element_type x1, other arithmetic, on_device(): scaled = (row_gates[:, None] * gathered_grad).astype(jnp.bfloat16)  10.4 us
    all_to_all x1, starting transfers between devices, on_device(): lax.all_to_all(slot_grad.reshape(owners, capacity, model_width), 'expert'...  9.54 us
  transfers between devices with their start and end apart: 6, of which 6 were waited for; matrix products, arithmetic and copies ran while one was open for 8% of the time, Pallas kernels for 0%

profile of v1, /device:TPU:1, one launch (start us, length us, event | category | flops | bytes accessed | tf_op | source)
XLA Modules:
  0.0 374.9 jit_solution(14969689032543285102)
XLA Ops:
  7.2 0.9 copy.51
  8.6 1.1 convolution_convert_fusion.3
  9.8 11.5 %all_to_all.44 = bf16[8,2,4096]{2,1,0:T(2,128)(2,1)} all-to-all(bf16[8,2,4096]{2,1,0:T(2,128)(2,1)S(1)} %reshape.94), channel_id=1, replica_groups=mesh['expert'=8,'replica_0'=4,'replica_1'=8] {'expert'}, dimensions={0} | all-to-all | bytes 262144 | tf_op jit(solution)/shard_map/all_to_all | solution.py:72
  21.3 1.1 convolution_convert_fusion.4
  22.5 9.2 %all_to_all.45 = bf16[8,2,4096]{2,1,0:T(2,128)(2,1)} all-to-all(bf16[8,2,4096]{2,1,0:T(2,128)(2,1)S(1)} %reshape.93), channel_id=1, replica_groups=mesh['expert'=8,'replica_0'=4,'replica_1'=8] {'expert'}, dimensions={0} | all-to-all | bytes 262144 | tf_op jit(solution)/shard_map/all_to_all | solution.py:73
  31.7 68.7 %all-gather.5.cloned.1.call-done = bf16[256,2,4096]{2,1,0:T(2,128)(2,1)} async-done(((bf16[8,2,4096]{2,1,0:T(2,128)(2,1)}), bf16[256,2,4096]{2,1,0:T(2,128)(2,1)}) %all-gather.5.cloned.1.call-update) | async-done | bytes 4194320 | tf_op jit(solution)/shard_map/all_gather | solution.py:79
  100.4 7.2 %reshape.95 = bf16[512,4096]{1,0:T(8,128)(2,1)} reshape(bf16[256,2,4096]{2,1,0:T(2,128)(2,1)} %all-gather.5.cloned.1.call-done) | data formatting | bytes 8388608 | tf_op jit(solution)/shard_map/reshape | solution.py:83
  107.6 4.3 %fusion.12 = f32[512,224]{0,1:T(8,128)S(1)} fusion(bf16[512,4096]{1,0:T(8,128)(2,1)} %reshape.95, bf16[1,224,4096]{2,1,0:T(8,128)(2,1)} %param.11), kind=kOutput, calls=%fused_computation.22 | convolution fusion | flops 939524096 | bytes 6488064 | tf_op jit(solution)/shard_map/dot_general | solution.py:84
  112.0 2.3 multiply_convert_fusion.5
  114.3 67.3 %all-gather.3.cloned.1.call-done = bf16[256,2,4096]{2,1,0:T(2,128)(2,1)} async-done(((bf16[8,2,4096]{2,1,0:T(2,128)(2,1)}), bf16[256,2,4096]{2,1,0:T(2,128)(2,1)}) %all-gather.3.cloned.1.call-update) | async-done | bytes 4194320 | tf_op jit(solution)/shard_map/all_gather | solution.py:80
  181.6 7.6 %reshape.98 = f32[512,4096]{1,0:T(8,128)} reshape(bf16[256,2,4096]{2,1,0:T(2,128)(2,1)} %all-gather.3.cloned.1.call-done) | data formatting | bytes 12582912 | tf_op jit(solution)/shard_map/convert_element_type | solution.py:92
  189.2 5.3 %multiply_reduce_fusion = f32[512]{0:T(512)S(1)} fusion(f32[512,4096]{1,0:T(8,128)} %reshape.98, bf16[512,224]{0,1:T(8,128)(2,1)S(1)} %get-tuple-element.19, bf16[1,224,4096]{2,1,0:T(8,128)(2,1)} %param.13), kind=kOutput, calls=%fused_computation.3 | convolution fusion | flops 943717888 | bytes 10455040 | tf_op jit(solution)/shard_map/dot_general | solution.py:91
  194.6 14.5 %all_to_all.46 = f32[32,1,16]{2,1,0:T(1,128)S(1)} all-to-all(f32[32,1,16]{2,1,0:T(1,128)S(1)} %bitcast.47), channel_id=1, replica_groups=mesh['expert'=8,'replica_0'=4,'replica_1'=8] {'replica_0','replica_1'}, dimensions={0} | all-to-all | bytes 4096 | tf_op jit(solution)/shard_map/all_to_all | solution.py:26
  209.1 0.7 all_to_all.32
  209.8 8.9 %all-to-all-start.3 = ((f32[8,1,2]{2,1,0:T(1,128)}), f32[8,1,2]{2,1,0:T(1,128)S(1)}, u32[]{:S(2)}, u32[]{:S(2)}) async-start(f32[8,1,2]{2,1,0:T(1,128)} %bitcast.4), calls=%async_computation.3 | async-start | bytes 8192 | tf_op jit(solution)/shard_map/all_to_all | solution.py:94
  218.8 4.4 %all-to-all-done.3 = f32[8,1,2]{2,1,0:T(1,128)S(1)} async-done(((f32[8,1,2]{2,1,0:T(1,128)}), f32[8,1,2]{2,1,0:T(1,128)S(1)}, u32[]{:S(2)}, u32[]{:S(2)}) %all-to-all-start.3) | async-done | bytes 96 | tf_op jit(solution)/shard_map/all_to_all | solution.py:94
  224.8 7.6 %all_to_all.47 = bf16[8,1,2]{2,1,0:T(2,128)(2,1)S(1)} all-to-all(bf16[8,1,2]{2,1,0:T(2,128)(2,1)S(1)} %convert_element_type.119), channel_id=1, replica_groups=mesh['expert'=8,'replica_0'=4,'replica_1'=8] {'expert'}, dimensions={0} | all-to-all | bytes 64 | tf_op jit(solution)/shard_map/all_to_all | solution.py:74
  232.5 11.6 %all_to_all.48 = bf16[32,8,2]{1,2,0:T(2,128)(2,1)S(1)} all-to-all(bf16[32,8,2]{1,2,0:T(2,128)(2,1)S(1)} %stack.5), channel_id=1, replica_groups=mesh['expert'=8,'replica_0'=4,'replica_1'=8] {'replica_0','replica_1'}, dimensions={0} | all-to-all | bytes 2048 | tf_op jit(solution)/shard_map/all_to_all | solution.py:14
  244.4 10.4 %multiply_convert_fusion.1 = bf16[256,2,4096]{2,1,0:T(2,128)(2,1)} fusion(f32[256,2]{1,0:T(8,128)S(1)} %bitcast.46, bf16[256,2,4096]{2,1,0:T(2,128)(2,1)} %all-gather.3.cloned.1.call-done), kind=kLoop, calls=%fused_computation.2 | loop fusion | flops 6291456 | bytes 8390656 | tf_op jit(solution)/shard_map/convert_element_type | solution.py:98
  254.8 7.2 %convert_element_type.105 = bf16[512,4096]{1,0:T(8,128)(2,1)} reshape(bf16[256,2,4096]{2,1,0:T(2,128)(2,1)} %multiply_convert_fusion.1) | data formatting | bytes 8388608 | tf_op jit(solution)/shard_map/convert_element_type | solution.py:98
  262.0 4.4 %multiply_convert_fusion.3 = (bf16[512,224]{0,1:T(8,128)(2,1)S(1)}, bf16[512,224]{0,1:T(8,128)(2,1)S(1)}) fusion(f32[512,224]{0,1:T(8,128)S(1)} %fusion.12, f32[512,224]{0,1:T(8,128)} %get-tuple-element.20, bf16[512,4096]{1,0:T(8,128)(2,1)} %convert_element_type.105, bf16[1,224,4096]{2,1,0:T(8,128)(2,1)} %param.13), kind=kOutput, calls=%fused_computation.24 | convolution fusion | flops 941015040 | bytes 7405568 | tf_op jit(solution)/shard_map/dot_general | solution.py:99
  266.4 1.3 fusion.10
  267.7 3.3 add_convert_fusion
  271.1 43.2 %reduce-scatter.3.cloned.1.call-done = bf16[128,4096]{1,0:T(8,128)(2,1)} async-done(((bf16[512,4096]{1,0:T(8,128)(2,1)}), bf16[128,4096]{1,0:T(8,128)(2,1)}) %reduce-scatter.3.cloned.1.call-update) | async-done | bytes 1048592 | tf_op jit(solution)/shard_map/reduce_scatter | solution.py:33
  315.2 4.5 %fusion.1 = bf16[1,224,4096]{2,1,0:T(8,128)(2,1)} fusion(bf16[512,224]{0,1:T(8,128)(2,1)S(1)} %get-tuple-element.17, bf16[512,4096]{1,0:T(8,128)(2,1)} %reshape.95), kind=kOutput, calls=%fused_computation.8 | convolution fusion | flops 940441600 | bytes 6258688 | tf_op jit(solution)/shard_map/dot_general | solution.py:110
  319.7 5.8 %fusion.2 = bf16[1,224,4096]{2,1,0:T(8,128)(2,1)} fusion(bf16[512,224]{0,1:T(8,128)(2,1)S(1)} %get-tuple-element.19, f32[512,4096]{1,0:T(8,128)} %reshape.98, f32[512]{0:T(512)S(1)} %reshape.100), kind=kOutput, calls=%fused_computation.9 | convolution fusion | flops 944635904 | bytes 10455040 | tf_op jit(solution)/shard_map/dot_general | solution.py:104
  325.5 25.5 %reduce-scatter.5.cloned.1.call-done = bf16[16,4096]{1,0:T(8,128)(2,1)} async-done(((bf16[128,4096]{1,0:T(8,128)(2,1)}), bf16[16,4096]{1,0:T(8,128)(2,1)}) %reduce-scatter.5.cloned.1.call-update) | async-done | bytes 131088 | tf_op jit(solution)/shard_map/reduce_scatter | solution.py:33
  351.1 1.6 reshape.96
  352.7 9.5 %all-to-all-start.6 = ((bf16[8,2,4096]{2,1,0:T(2,128)(2,1)}), bf16[8,2,4096]{2,1,0:T(2,128)(2,1)S(1)}, u32[]{:S(2)}, u32[]{:S(2)}) async-start(bf16[8,2,4096]{2,1,0:T(2,128)(2,1)} %reshape.96), calls=%async_computation.8 | async-start | bytes 262144 | tf_op jit(solution)/shard_map/all_to_all | solution.py:118
  362.2 4.5 %fusion = bf16[1,224,4096]{2,1,0:T(8,128)(2,1)} fusion(bf16[512,224]{0,1:T(8,128)(2,1)S(1)} %get-tuple-element.18, bf16[512,4096]{1,0:T(8,128)(2,1)} %reshape.95), kind=kOutput, calls=%fused_computation.7 | convolution fusion | flops 940441600 | bytes 6258688 | tf_op jit(solution)/shard_map/dot_general | solution.py:107
  366.8 0.7 all-to-all-done.6
  367.5 0.8 convolution_convert_fusion.5
  (38 shorter events, 3.8 us)
Async XLA Ops:
  7.2 104.8 %copy-start = (bf16[1,224,4096]{2,1,0:T(8,128)(2,1)S(1)}, bf16[1,224,4096]{2,1,0:T(8,128)(2,1)}, u32[]{:S(2)}) copy-start(bf16[1,224,4096]{2,1,0:T(8,128)(2,1)} %param.12) | copy-start | bytes 5505028
  7.2 93.2 %all-gather.5.cloned.1.call-start = ((), (), s32[]{:S(2)}) async-start(), calls=%async_computation.10 | async-start | bytes 4325376 | tf_op jit(solution)/shard_map/all_gather | solution.py:79
  21.3 160.3 %all-gather.3.cloned.1.call-start = ((), (), s32[]{:S(2)}) async-start(), calls=%async_computation.9 | async-start | bytes 4325376 | tf_op jit(solution)/shard_map/all_gather | solution.py:80
  107.6 4.4 %copy-start.1 = (bf16[512,4096]{1,0:T(8,128)(2,1)S(1)}, bf16[512,4096]{1,0:T(8,128)(2,1)}, u32[]{:S(2)}) copy-start(bf16[512,4096]{1,0:T(8,128)(2,1)} %reshape.95) | copy-start | bytes 12582916
  189.2 29.6 %copy-start.3 = (f32[6,2]{0,1:T(2,128)S(1)}, f32[6,2]{0,1:T(2,128)}, u32[]{:S(2)}) copy-start(f32[6,2]{0,1:T(2,128)} %param.10) | copy-start | bytes 148
  209.8 13.5 %all-to-all-start.3 = ((f32[8,1,2]{2,1,0:T(1,128)}), f32[8,1,2]{2,1,0:T(1,128)S(1)}, u32[]{:S(2)}, u32[]{:S(2)}) async-start(f32[8,1,2]{2,1,0:T(1,128)} %bitcast.4), calls=%async_computation.3 | async-start | bytes 8192 | tf_op jit(solution)/shard_map/all_to_all | solution.py:94
  218.7 95.6 %reduce-scatter.3.cloned.1.call-start = ((), (), s32[]{:S(2)}) async-start(), calls=%async_computation.11 | async-start | bytes 5242880 | tf_op jit(solution)/shard_map/reduce_scatter | solution.py:33
  262.0 4.5 %copy-start.2 = (bf16[1,224,4096]{2,1,0:T(8,128)(2,1)S(1)}, bf16[1,224,4096]{2,1,0:T(8,128)(2,1)}, u32[]{:S(2)}) copy-start(bf16[1,224,4096]{2,1,0:T(8,128)(2,1)} %param.11) | copy-start | bytes 5505028
  271.1 80.0 %reduce-scatter.5.cloned.1.call-start = ((), (), s32[]{:S(2)}) async-start(), calls=%async_computation.12 | async-start | bytes 1179648 | tf_op jit(solution)/shard_map/reduce_scatter | solution.py:33
  352.7 14.8 %all-to-all-start.6 = ((bf16[8,2,4096]{2,1,0:T(2,128)(2,1)}), bf16[8,2,4096]{2,1,0:T(2,128)(2,1)S(1)}, u32[]{:S(2)}, u32[]{:S(2)}) async-start(bf16[8,2,4096]{2,1,0:T(2,128)(2,1)} %reshape.96), calls=%async_computation.8 | async-start | bytes 262144 | tf_op jit(solution)/shard_map/all_to_all | solution.py:118
Sparse Core Ops, SparseCore 0:
  21.4 78.9 all-gather.4
  103.0 78.5 all-gather.2
  271.2 43.1 reduce-scatter.2
  316.8 34.2 reduce-scatter.4
